TPU v7x, 256 devices: a whole 4x4x8 slice. The times are simulated.
256 devices in a mesh: row: 16 (over z_lo, x), col: 4 (over z_hi, core), depth: 4 (over y).
Axes of the slice: x: 4, y: 4, z: 8 (z_hi: 2, z_lo: 4; z = z_hi * 4 + z_lo), core: 2. Of those that a mesh axis runs over, the one named last changes fastest.
Arguments:
- inputs: bfloat16 [1024, 5120], P(('row', 'depth'), 'col'), may hold values from -6 to 6
- targets: bfloat16 [1024, 5120], P(('row', 'depth'), 'col'), may hold values from -6 to 6
- norm_gain: float32 [5120], P('col'), may hold values from 0.5 to 1.5
- w_gate: bfloat16 [5120, 8192], P('col', ('row', 'depth')), may hold values from -0.078125 to 0.078125
- w_up: bfloat16 [5120, 8192], P('col', ('row', 'depth')), may hold values from -0.078125 to 0.078125
- w_down: bfloat16 [8192, 5120], P(('row', 'depth'), 'col'), may hold values from -0.0625 to 0.0625
- probe_gate: bfloat16 [5120, 8192], P('col', ('row', 'depth')), may hold values from -1 to 1, as said below
- probe_up: bfloat16 [5120, 8192], P('col', ('row', 'depth')), may hold values from -1 to 1, as said below
- probe_down: bfloat16 [8192, 5120], P(('row', 'depth'), 'col'), may hold values from -1 to 1, as said below
- moment_gate: float32 [5120, 8192], P('col', ('row', 'depth')), may hold values from -18 to 18
- moment_up: float32 [5120, 8192], P('col', ('row', 'depth')), may hold values from -18 to 18
- moment_down: float32 [8192, 5120], P(('row', 'depth'), 'col'), may hold values from -18 to 18
- second_gate: float32 [5120, 8192], P('col', ('row', 'depth')), may hold values from 1 to 100
- second_up: float32 [5120, 8192], P('col', ('row', 'depth')), may hold values from 1 to 100
- second_down: float32 [8192, 5120], P(('row', 'depth'), 'col'), may hold values from 1 to 100
Outputs:
- new_moment_gate: float32 [5120, 8192], P('col', ('row', 'depth'))
- new_moment_up: float32 [5120, 8192], P('col', ('row', 'depth'))
- new_moment_down: float32 [8192, 5120], P(('row', 'depth'), 'col')
- new_second_gate: float32 [5120, 8192], P('col', ('row', 'depth'))
- new_second_up: float32 [5120, 8192], P('col', ('row', 'depth'))
- new_second_down: float32 [8192, 5120], P(('row', 'depth'), 'col')
- step_gate: float32 [5120, 8192], P('col', ('row', 'depth'))
- step_up: float32 [5120, 8192], P('col', ('row', 'depth'))
- step_down: float32 [8192, 5120], P(('row', 'depth'), 'col')
Inputs may be any that keep to these rules, and one draw needn't show every extreme that they name: `probe_gate`: every entry is +1 or -1. `probe_up`: every entry is +1 or -1. `probe_down`: every entry is +1 or -1.
All inputs are finite; a program needn't handle non-finite values.
Results may differ from a plain program's by a relative error of at most 0.0046.
Values may be sent and summed in bfloat16 or wider, within the bound.
No kernel may reach another device: no remote copies, remote signals or barrier semaphores. Data moves between devices by JAX's collectives and lax.ppermute only.
A program may use at most 128 MiB of HBM per device.

v0:
```python
import jax
import jax.numpy as jnp
from jax import lax
from jax.sharding import PartitionSpec as P

D = 5120
TILE = 128
STEP = 1000
beta_one = 0.9
beta_two = 0.999
adam_floor = 1e-08
norm_floor = 1e-05


def copy_for_each(value, axis):
    count = lax.axis_size(axis)
    return lax.all_to_all(
        jnp.broadcast_to(value[None], (count, *value.shape)), axis, 0, 0, tiled=True
    )


def of_everyone(value, axis):
    everything = copy_for_each(value, axis)
    return jnp.sum(everything, axis=0)


def cut_along(value, dim, count):
    before, after = (value.shape[:dim], value.shape[dim + 1 :])
    return jnp.moveaxis(value.reshape(*before, count, -1, *after), dim, 0)


def sent_and_summed(value, axis, dim):
    blocks = cut_along(value, dim, lax.axis_size(axis))
    arrived = lax.all_to_all(blocks, axis, split_axis=0, concat_axis=0, tiled=True)
    return arrived.sum(axis=0)


def sent_together(arrays, axis, dim, along):
    widths = [a.shape[along] for a in arrays]
    both = jnp.concatenate(arrays, axis=along)
    result = lax.all_gather(both, axis, axis=dim, tiled=True)
    return tuple(jnp.split(result, [sum(widths[:k]) for k in range(1, len(widths))], axis=along))


def in_one(arrays, axis):
    ends = [0]
    for a in arrays:
        ends.append(ends[-1] + a.size)
    so_far = of_everyone(jnp.concatenate([a.ravel() for a in arrays]), axis)
    return tuple((so_far[b:e].reshape(a.shape) for a, b, e in zip(arrays, ends, ends[1:])))


def silu_parts(gate_pre):
    sig = jax.nn.sigmoid(gate_pre)
    act = gate_pre * sig
    slope = sig * (1.0 + gate_pre * (1.0 - sig))
    bend = sig * (1.0 - sig) * (2.0 + gate_pre * (1.0 - 2.0 * sig))
    return (act, slope, bend)


def tile_means(product):
    height, breadth = product.shape
    blocks = product.reshape(height // TILE, TILE, breadth // TILE, TILE)
    means = jnp.mean(blocks, axis=(1, 3), keepdims=True)
    return jnp.broadcast_to(means, blocks.shape).reshape(height, breadth)


def adahessian(moment, second, gradient, curvature, probe):
    averaged = tile_means(probe.astype(jnp.float32) * curvature)
    new_moment = beta_one * moment + (1.0 - beta_one) * gradient
    new_second = beta_two * second + (1.0 - beta_two) * averaged * averaged
    corrected = new_moment / (1.0 - beta_one**STEP)
    scale_root = jnp.sqrt(new_second / (1.0 - beta_two**STEP))
    return (new_moment, new_second, corrected / (scale_root + adam_floor))


def matmul(left, right):
    return jnp.dot(left, right, preferred_element_type=jnp.float32)


def inner_left(left, right):
    return lax.dot_general(
        left, right, (((0,), (0,)), ((), ())), preferred_element_type=jnp.float32
    )


def inner_right(left, right):
    return lax.dot_general(
        left, right, (((1,), (1,)), ((), ())), preferred_element_type=jnp.float32
    )


def shards(
    inputs,
    targets,
    norm_gain,
    w_gate,
    w_up,
    w_down,
    probe_gate,
    probe_up,
    probe_down,
    moment_gate,
    moment_up,
    moment_down,
    second_gate,
    second_up,
    second_down,
):
    feats = inputs.astype(jnp.float32)
    shard_rows = feats.shape[0]
    local_width = feats.shape[1]
    squares = of_everyone(jnp.sum(feats * feats, axis=1), "col")
    scaling = lax.rsqrt(squares / D + norm_floor)
    normed_rows = (feats * scaling[:, None] * norm_gain).astype(jnp.bfloat16)
    normed = lax.all_gather(normed_rows, ("row", "depth"), axis=0, tiled=True)
    total_rows = normed.shape[0]
    gate_pre, up_pre, gate_tan, up_tan = lax.psum(
        (
            matmul(normed, w_gate),
            matmul(normed, w_up),
            matmul(normed, probe_gate),
            matmul(normed, probe_up),
        ),
        "col",
    )
    act, slope, bend = silu_parts(gate_pre)
    hidden = (act * up_pre).astype(jnp.bfloat16)
    hidden_tan = (slope * gate_tan * up_pre + act * up_tan).astype(jnp.bfloat16)
    row_count = lax.axis_size("row")
    depth_count = lax.axis_size("depth")
    primal = matmul(hidden, w_down)
    tangent = matmul(hidden_tan, w_down) + matmul(hidden, probe_down)
    whole_terms = jnp.concatenate([primal, tangent], axis=1).reshape(
        row_count, depth_count * shard_rows, 2 * local_width
    )
    layered = lax.psum_scatter(whole_terms, "depth", scatter_dimension=1, tiled=True)
    summed = sent_and_summed(layered, "row", 0).reshape(shard_rows, 2 * local_width)
    outputs = summed[:, :local_width] + feats
    error_rows = (outputs - targets.astype(jnp.float32)).astype(jnp.bfloat16)
    tangent_rows = summed[:, local_width:].astype(jnp.bfloat16)
    grid_error, grid_tan = sent_together(
        (
            error_rows.reshape(1, shard_rows, local_width),
            tangent_rows.reshape(1, shard_rows, local_width),
        ),
        "row",
        0,
        1,
    )
    layer_error, layer_tan = sent_together((grid_error, grid_tan), "depth", 1, 0)
    error = layer_error.reshape(total_rows, local_width)
    error_tan = layer_tan.reshape(total_rows, local_width)
    back_hidden, back_tan = in_one(
        (
            inner_right(error, w_down),
            inner_right(error_tan, w_down) + inner_right(error, probe_down),
        ),
        "col",
    )
    back_gate = (back_hidden * up_pre * slope).astype(jnp.bfloat16)
    back_up = (back_hidden * act).astype(jnp.bfloat16)
    gate_tan_back = (
        back_tan * up_pre * slope
        + back_hidden * up_tan * slope
        + back_hidden * up_pre * bend * gate_tan
    ).astype(jnp.bfloat16)
    up_tan_back = (back_tan * act + back_hidden * slope * gate_tan).astype(jnp.bfloat16)
    grad_gate = inner_left(normed, back_gate)
    grad_up = inner_left(normed, back_up)
    grad_down = inner_left(hidden, error)
    curve_gate = inner_left(normed, gate_tan_back)
    curve_up = inner_left(normed, up_tan_back)
    curve_down = inner_left(hidden_tan, error) + inner_left(hidden, error_tan)
    gate_moment, gate_second, gate_step = adahessian(
        moment_gate, second_gate, grad_gate, curve_gate, probe_gate
    )
    up_moment, up_second, up_step = adahessian(moment_up, second_up, grad_up, curve_up, probe_up)
    down_moment, down_second, down_step = adahessian(
        moment_down, second_down, grad_down, curve_down, probe_down
    )
    return (
        gate_moment,
        up_moment,
        down_moment,
        gate_second,
        up_second,
        down_second,
        gate_step,
        up_step,
        down_step,
    )


def solution(mesh):
    return jax.shard_map(
        shards,
        mesh=mesh,
        in_specs=(
            P(("row", "depth"), "col"),
            P(("row", "depth"), "col"),
            P("col"),
            P("col", ("row", "depth")),
            P("col", ("row", "depth")),
            P(("row", "depth"), "col"),
            P("col", ("row", "depth")),
            P("col", ("row", "depth")),
            P(("row", "depth"), "col"),
            P("col", ("row", "depth")),
            P("col", ("row", "depth")),
            P(("row", "depth"), "col"),
            P("col", ("row", "depth")),
            P("col", ("row", "depth")),
            P(("row", "depth"), "col"),
        ),
        out_specs=(
            P("col", ("row", "depth")),
            P("col", ("row", "depth")),
            P(("row", "depth"), "col"),
            P("col", ("row", "depth")),
            P("col", ("row", "depth")),
            P(("row", "depth"), "col"),
            P("col", ("row", "depth")),
            P("col", ("row", "depth")),
            P(("row", "depth"), "col"),
        ),
        check_vma=False,
    )
```

profile of v0, /device:TPU:2, one launch (start us, length us, event | category | flops | bytes accessed | tf_op | source)
XLA Modules:
  0.0 945.6 jit_solution(12996763994163332832)
XLA Ops:
  7.2 1.0 fusion.20
  8.2 15.9 %all_to_all.17 = f32[4,1,16]{2,1,0:T(1,128)S(1)} all-to-all(f32[4,1,16]{2,1,0:T(1,128)S(1)} %broadcast_in_dim.44), channel_id=1, replica_groups=mesh['row'=16,'col'=4,'depth'=4] {'col'}, dimensions={0} | all-to-all | bytes 512 | tf_op jit(solution)/shard_map/all_to_all | solution.py:17
  24.2 1.5 fusion.22
  25.8 342.4 %all-gather.4.cloned.1.call-done = bf16[1024,1280]{1,0:T(8,128)(2,1)} async-done(((bf16[16,1280]{1,0:T(8,128)(2,1)}), bf16[1024,1280]{1,0:T(8,128)(2,1)}) %all-gather.4.cloned.1.call-update) | async-done | bytes 2621456 | tf_op jit(solution)/shard_map/all_gather | solution.py:116
  368.1 3.5 fusion.36
  371.7 1.6 fusion.37
  373.3 1.6 fusion.39
  375.0 1.6 fusion.40
  376.7 99.8 %all-reduce.3.cloned.1.call-done = (f32[1024,128]{1,0:T(8,128)}, f32[1024,128]{1,0:T(8,128)}, f32[1024,128]{1,0:T(8,128)}, f32[1024,128]{1,0:T(8,128)}) async-done(((f32[1024,128]{1,0:T(8,128)}, f32[1024,128]{1,0:T(8,128)}, f32[1024,128]{1,0:T(8,128)}, f32[1024,128]{1,0:T(8,128)}), (f32[1024,128]{1,0:T(8,128)}, f32[1024,128]{1,0:T(8,128)}, f32[1024,128]{1,0:T(8,128)}, ...) | async-done | bytes 2097168 | tf_op jit(solution)/shard_map/psum | solution.py:118
  476.5 1.8 multiply_convert_fusion.2
  479.2 3.1 fusion.38
  482.3 3.2 convolution_add_fusion
  485.5 9.2 pad_maximum_fusion
  494.8 101.7 %reduce-scatter.2.cloned.1.call-done = f32[16,16,2560]{2,1,0:T(8,128)} async-done(((f32[16,64,2560]{2,1,0:T(8,128)}), f32[16,16,2560]{2,1,0:T(8,128)}) %reduce-scatter.2.cloned.1.call-update) | async-done | bytes 2621456 | tf_op jit(solution)/shard_map/reduce_scatter | solution.py:137
  596.5 66.4 %all_to_all.18 = f32[16,1,16,2560]{3,2,1,0:T(8,128)S(1)} all-to-all(f32[16,1,16,2560]{3,2,1,0:T(8,128)} %bitcast.101), channel_id=1, replica_groups=mesh['row'=16,'col'=4,'depth'=4] {'row'}, dimensions={0} | all-to-all | bytes 5242880 | tf_op jit(solution)/shard_map/all_to_all | solution.py:34
  664.6 0.9 fusion.26
  666.2 78.4 %all-gather.6.cloned.1.call-done = bf16[16,32,1280]{2,1,0:T(8,128)(2,1)} async-done(((bf16[1,32,1280]{2,1,0:T(8,128)(2,1)}), bf16[16,32,1280]{2,1,0:T(8,128)(2,1)}) %all-gather.6.cloned.1.call-update) | async-done | bytes 1310736 | tf_op jit(solution)/shard_map/all_gather | solution.py:41
  744.6 1.4 fusion.35
  746.0 1.2 pad_maximum_fusion.1
  747.2 58.2 %all-gather.8.cloned.1.call-done = bf16[32,64,1280]{2,1,0:T(8,128)(2,1)} async-done(((bf16[32,16,1280]{2,1,0:T(8,128)(2,1)}), bf16[32,64,1280]{2,1,0:T(8,128)(2,1)}) %all-gather.8.cloned.1.call-update) | async-done | bytes 5242896 | tf_op jit(solution)/shard_map/all_gather | solution.py:41
  805.4 2.9 fusion.34
  811.7 4.6 broadcast_in_dim.45
  816.3 7.0 all-to-all-start.2
  823.3 1.9 copy.33
  825.2 1.9 copy.32
  827.7 1.2 copy-done.5
  830.1 2.0 add_divide_fusion
  832.2 87.5 %all-to-all-done.2 = f32[4,1,262144]{2,1,0:T(1,128)} async-done(((f32[4,1,262144]{2,1,0:T(1,128)}), f32[4,1,262144]{2,1,0:T(1,128)}, u32[]{:S(2)}, u32[]{:S(2)}) %all-to-all-start.2) | async-done | bytes 4194336 | tf_op jit(solution)/shard_map/all_to_all | solution.py:17
  919.7 10.8 %reduce_sum.87 = f32[262144]{0:T(1024)} reduce(f32[4,1,262144]{2,1,0:T(1,128)} %all-to-all-done.2, f32[]{:T(128)} %constant.13.clone.1), dimensions={0,1}, to_apply=%region_8.0 | reduce | flops 786432 | bytes 5242884 | tf_op jit(solution)/shard_map/reduce_sum | solution.py:24
  930.5 2.2 fusion.7
  934.3 2.4 add_divide_fusion.1
  936.6 2.4 add_divide_fusion.2
  (84 shorter events, 10.2 us)
Async XLA Ops:
  7.2 471.2 %copy-start = (bf16[128,1280]{1,0:T(8,128)(2,1)S(1)}, bf16[128,1280]{1,0:T(8,128)(2,1)}, u32[]{:S(2)}) copy-start(bf16[128,1280]{1,0:T(8,128)(2,1)} %param.20) | copy-start | bytes 983044
  7.2 364.5 %copy-start.19 = (bf16[1280,128]{1,0:T(8,128)(2,1)S(1)}, bf16[1280,128]{1,0:T(8,128)(2,1)}, u32[]{:S(2)}) copy-start(bf16[1280,128]{1,0:T(8,128)(2,1)} %param.19) | copy-start | bytes 983044
  7.2 360.9 %all-gather.4.cloned.1.call-start = ((), (), s32[]{:S(2)}) async-start(), calls=%async_computation.4 | async-start | bytes 2662400 | tf_op jit(solution)/shard_map/all_gather | solution.py:116
  25.7 450.8 %all-reduce.3.cloned.1.call-start = ((), (), s32[]{:S(2)}) async-start(), calls=%async_computation.8 | async-start | bytes 4194304 | tf_op jit(solution)/shard_map/psum | solution.py:118
  368.1 3.6 copy-start.2
  371.7 1.6 copy-start.10
  373.3 1.6 copy-start.9
  376.6 219.8 %reduce-scatter.2.cloned.1.call-start = ((), (), s32[]{:S(2)}) async-start(), calls=%async_computation.5 | async-start | bytes 13107200 | tf_op jit(solution)/shard_map/reduce_scatter | solution.py:137
  479.2 3.1 copy-start.6
  494.7 249.9 %all-gather.6.cloned.1.call-start = ((), (), s32[]{:S(2)}) async-start(), calls=%async_computation.6 | async-start | bytes 1392640 | tf_op jit(solution)/shard_map/all_gather | solution.py:41
  662.9 1.7 copy-start.18
  662.9 1.7 copy-start.21
  666.1 139.3 %all-gather.8.cloned.1.call-start = ((), (), s32[]{:S(2)}) async-start(), calls=%async_computation.7 | async-start | bytes 6553600 | tf_op jit(solution)/shard_map/all_gather | solution.py:41
  808.3 1.6 copy-start.4
  809.8 1.0 copy-start.7
  816.3 103.4 %all-to-all-start.2 = ((f32[4,1,262144]{2,1,0:T(1,128)}), f32[4,1,262144]{2,1,0:T(1,128)}, u32[]{:S(2)}, u32[]{:S(2)}) async-start(f32[4,1,262144]{2,1,0:T(1,128)} %broadcast_in_dim.45), calls=%async_computation.3 | async-start | bytes 8388608 | tf_op jit(solution)/shard_map/all_to_all | solution.py:17
  823.3 4.3 copy-start.8
  827.1 1.7 copy-start.5
  828.8 1.1 copy-start.12
  828.8 1.3 copy-start.13
  832.2 98.3 %copy-start.3 = (bf16[1024,1280]{1,0:T(8,128)(2,1)S(1)}, bf16[1024,1280]{1,0:T(8,128)(2,1)}, u32[]{:S(2)}) copy-start(bf16[1024,1280]{1,0:T(8,128)(2,1)} %all-gather.4.cloned.1.call-done) | copy-start | bytes 7864324
  832.2 98.3 %copy-start.15 = (f32[1024,128]{1,0:T(8,128)S(1)}, f32[1024,128]{1,0:T(8,128)}, u32[]{:S(2)}) copy-start(f32[1024,128]{1,0:T(8,128)} %get-tuple-element.12) | copy-start | bytes 1572868
  930.5 2.5 copy-start.11
  930.5 2.5 copy-start.14
  930.5 2.5 copy-start.16
  930.5 2.5 copy-start.17
  930.5 2.5 copy-start.20
  933.0 1.1 copy-start.22
  933.0 1.3 copy-start.23
  934.3 2.4 copy-start.24
  934.3 2.4 copy-start.25
  936.6 2.4 copy-start.1
Sparse Core Ops, SparseCore 0:
  25.8 342.2 all-gather.3
  376.8 99.7 all-reduce.2
  494.8 101.5 reduce-scatter.1
  666.3 78.3 all-gather.5
  747.3 57.9 all-gather.7
where the time goes:
time: 946 us
  waiting for transfers between devices  768 us (81%)
  blocking collectives  82.3 us (9%)
  matrix products  29.1 us (3%)
  other arithmetic  28.5 us (3%)
  local copies, waits for them, and re-layouts  16.4 us (2%)
  between operations  14 us (1%)
    all_gather x1, waiting for transfers between devices, shards(): normed = lax.all_gather(normed_rows, ('row', 'depth'), axis=0, tiled=True)  342 us
    all_gather x2, waiting for transfers between devices, sent_together(): result = lax.all_gather(both, axis, axis=dim, tiled=True)  137 us
    reduce_scatter x1, waiting for transfers between devices, shards(): lax.psum_scatter(whole_terms, 'depth', scatter_dimension=1, tiled=True)  102 us
    psum x1, waiting for transfers between devices, shards(): lax.psum((matmul(normed, w_gate), matmul(normed, w_up), matmul(normed, pr...  99.8 us
    all_to_all x1, waiting for transfers between devices, copy_for_each(): lax.all_to_all(jnp.broadcast_to(value[None], (count, *value.shape)), axis...  87.5 us
    all_to_all x1, blocking collectives, sent_and_summed(): lax.all_to_all(blocks, axis, split_axis=0, concat_axis=0, tiled=True)  66.4 us
  transfers between devices with their start and end apart: 6, of which 6 were waited for; matrix products, arithmetic and copies ran while one was open for 1% of the time, Pallas kernels for 0%

commit v1 on v0

--- a/solution.py
+++ b/solution.py
@@ -113,7 +113,12 @@
     squares = of_everyone(jnp.sum(feats * feats, axis=1), "col")
     scaling = lax.rsqrt(squares / D + norm_floor)
     normed_rows = (feats * scaling[:, None] * norm_gain).astype(jnp.bfloat16)
-    normed = lax.all_gather(normed_rows, ("row", "depth"), axis=0, tiled=True)
+    normed = jnp.concatenate(
+        lax.all_to_all(
+            jnp.stack([normed_rows] * lax.axis_size(("row", "depth"))), ("row", "depth"), 0, 0
+        ),
+        axis=0,
+    )
     total_rows = normed.shape[0]
     gate_pre, up_pre, gate_tan, up_tan = lax.psum(
         (

time: 946 us -> 665 us (0.70)
  waiting for transfers between devices: 768 us -> 416 us
  blocking collectives: 82.3 us -> 152 us
    all_gather x1 -> x0, waiting for transfers between devices: 342 us -> none  [shards(): normed = lax.all_gather(normed_rows, ('row', 'depth'), axis=0, tiled=True)]
    all_to_all x0 -> x1, blocking collectives: none -> 70 us  [shards(): lax.all_to_all(jnp.stack([normed_rows] * lax.axis_size(('row', 'depth')))...]
  transfers between devices with their start and end apart: 6 -> 5, of which waited for: 6 -> 5; matrix products, arithmetic and copies ran while one was open for 1% -> 1% of each run, Pallas kernels for 0% -> 0%
where the time goes in v1:
time: 665 us
  waiting for transfers between devices  416 us (63%)
  blocking collectives  152 us (23%)
  other arithmetic  29.6 us (4%)
  matrix products  29.1 us (4%)
  local copies, waits for them, and re-layouts  16.3 us (2%)
  between operations  14 us (2%)
  starting transfers between devices  7.17 us (1%)
    all_gather x2, waiting for transfers between devices, sent_together(): result = lax.all_gather(both, axis, axis=dim, tiled=True)  137 us
    reduce_scatter x1, waiting for transfers between devices, shards(): lax.psum_scatter(whole_terms, 'depth', scatter_dimension=1, tiled=True)  102 us
    psum x1, waiting for transfers between devices, shards(): lax.psum((matmul(normed, w_gate), matmul(normed, w_up), matmul(normed, pr...  91.7 us
    all_to_all x1, waiting for transfers between devices, copy_for_each(): lax.all_to_all(jnp.broadcast_to(value[None], (count, *value.shape)), axis...  86.1 us
    all_to_all x1, blocking collectives, shards(): lax.all_to_all(jnp.stack([normed_rows] * lax.axis_size(('row', 'depth')))...  70 us
    all_to_all x1, blocking collectives, sent_and_summed(): lax.all_to_all(blocks, axis, split_axis=0, concat_axis=0, tiled=True)  66.5 us
    all_to_all x1, blocking collectives, copy_for_each(): lax.all_to_all(jnp.broadcast_to(value[None], (count, *value.shape)), axis...  15.9 us
    dot_general x7, matrix products, matmul(): return jnp.dot(left, right, preferred_element_type=jnp.float32)  13.6 us
  transfers between devices with their start and end apart: 5, of which 5 were waited for; matrix products, arithmetic and copies ran while one was open for 1% of the time, Pallas kernels for 0%

profile of v1, /device:TPU:2, one launch (start us, length us, event | category | flops | bytes accessed | tf_op | source)
XLA Modules:
  0.0 664.7 jit_solution(411793362196336059)
XLA Ops:
  7.2 0.9 fusion.20
  8.2 15.9 %all_to_all.22 = f32[4,1,16]{2,1,0:T(1,128)S(1)} all-to-all(f32[4,1,16]{2,1,0:T(1,128)S(1)} %broadcast_in_dim.44), channel_id=1, replica_groups=mesh['row'=16,'col'=4,'depth'=4] {'col'}, dimensions={0} | all-to-all | bytes 512 | tf_op jit(solution)/shard_map/all_to_all | solution.py:17
  25.2 70.0 %all_to_all.23 = bf16[64,16,1280]{2,1,0:T(8,128)(2,1)S(1)} all-to-all(bf16[64,16,1280]{2,1,0:T(8,128)(2,1)S(1)} %stack.2), channel_id=1, replica_groups=mesh['row'=16,'col'=4,'depth'=4] {'row','depth'}, dimensions={0} | all-to-all | bytes 5242880 | tf_op jit(solution)/shard_map/all_to_all | solution.py:117
  95.2 1.6 fusion.36
  96.9 1.6 fusion.37
  98.5 1.6 fusion.39
  100.2 1.6 fusion.40
  101.9 91.7 %all-reduce.3.cloned.1.call-done = (f32[1024,128]{1,0:T(8,128)}, f32[1024,128]{1,0:T(8,128)}, f32[1024,128]{1,0:T(8,128)}, f32[1024,128]{1,0:T(8,128)}) async-done(((f32[1024,128]{1,0:T(8,128)}, f32[1024,128]{1,0:T(8,128)}, f32[1024,128]{1,0:T(8,128)}, f32[1024,128]{1,0:T(8,128)}), (f32[1024,128]{1,0:T(8,128)}, f32[1024,128]{1,0:T(8,128)}, f32[1024,128]{1,0:T(8,128)}, ...) | async-done | bytes 2097168 | tf_op jit(solution)/shard_map/psum | solution.py:123
  193.5 1.8 multiply_convert_fusion.2
  196.2 3.1 fusion.38
  199.3 3.2 convolution_add_fusion
  202.5 9.2 %pad_maximum_fusion = f32[1024,2560]{1,0:T(8,128)} fusion(f32[1024,1280]{1,0:T(8,128)} %convolution_add_fusion, f32[1024,1280]{1,0:T(8,128)} %fusion.38), kind=kLoop, calls=%fused_computation.1 | loop fusion | flops 2621440 | bytes 20971520 | tf_op jit(solution)/shard_map/concatenate | solution.py:139
  211.8 101.7 %reduce-scatter.2.cloned.1.call-done = f32[16,16,2560]{2,1,0:T(8,128)} async-done(((f32[16,64,2560]{2,1,0:T(8,128)}), f32[16,16,2560]{2,1,0:T(8,128)}) %reduce-scatter.2.cloned.1.call-update) | async-done | bytes 2621456 | tf_op jit(solution)/shard_map/reduce_scatter | solution.py:142
  313.5 66.5 %all_to_all.24 = f32[16,1,16,2560]{3,2,1,0:T(8,128)} all-to-all(f32[16,1,16,2560]{3,2,1,0:T(8,128)} %bitcast.110), channel_id=1, replica_groups=mesh['row'=16,'col'=4,'depth'=4] {'row'}, dimensions={0} | all-to-all | bytes 5242880 | tf_op jit(solution)/shard_map/all_to_all | solution.py:34
  380.0 2.6 reduce_sum.86
  385.1 78.4 %all-gather.3.cloned.1.call-done = bf16[16,32,1280]{2,1,0:T(8,128)(2,1)} async-done(((bf16[1,32,1280]{2,1,0:T(8,128)(2,1)}), bf16[16,32,1280]{2,1,0:T(8,128)(2,1)}) %all-gather.3.cloned.1.call-update) | async-done | bytes 1310736 | tf_op jit(solution)/shard_map/all_gather | solution.py:41
  463.5 1.4 fusion.35
  464.9 1.2 pad_maximum_fusion.1
  466.1 58.2 %all-gather.5.cloned.1.call-done = bf16[32,64,1280]{2,1,0:T(8,128)(2,1)} async-done(((bf16[32,16,1280]{2,1,0:T(8,128)(2,1)}), bf16[32,64,1280]{2,1,0:T(8,128)(2,1)}) %all-gather.5.cloned.1.call-update) | async-done | bytes 5242896 | tf_op jit(solution)/shard_map/all_gather | solution.py:41
  524.3 2.9 fusion.34
  530.8 4.6 broadcast_in_dim.45
  535.4 7.0 %all-to-all-start.3 = ((f32[4,1,262144]{2,1,0:T(1,128)}), f32[4,1,262144]{2,1,0:T(1,128)}, u32[]{:S(2)}, u32[]{:S(2)}) async-start(f32[4,1,262144]{2,1,0:T(1,128)} %broadcast_in_dim.45), calls=%async_computation.4 | async-start | bytes 8388608 | tf_op jit(solution)/shard_map/all_to_all | solution.py:17
  542.4 1.9 copy.33
  544.3 1.9 copy.32
  546.2 2.4 fusion.43
  549.5 1.0 copy-done.3
  550.7 2.1 add_divide_fusion
  552.7 86.1 %all-to-all-done.3 = f32[4,1,262144]{2,1,0:T(1,128)} async-done(((f32[4,1,262144]{2,1,0:T(1,128)}), f32[4,1,262144]{2,1,0:T(1,128)}, u32[]{:S(2)}, u32[]{:S(2)}) %all-to-all-start.3) | async-done | bytes 4194336 | tf_op jit(solution)/shard_map/all_to_all | solution.py:17
  638.8 10.8 %reduce_sum.87 = f32[262144]{0:T(1024)} reduce(f32[4,1,262144]{2,1,0:T(1,128)} %all-to-all-done.3, f32[]{:T(128)} %constant.13.clone.1), dimensions={0,1}, to_apply=%region_8.0 | reduce | flops 786432 | bytes 5242884 | tf_op jit(solution)/shard_map/reduce_sum | solution.py:24
  649.6 2.2 fusion.7
  653.4 2.4 add_divide_fusion.1
  655.7 2.4 add_divide_fusion.2
  (85 shorter events, 10.7 us)
Async XLA Ops:
  7.2 188.2 %copy-start = (bf16[128,1280]{1,0:T(8,128)(2,1)S(1)}, bf16[128,1280]{1,0:T(8,128)(2,1)}, u32[]{:S(2)}) copy-start(bf16[128,1280]{1,0:T(8,128)(2,1)} %param.20) | copy-start | bytes 983044
  7.2 186.4 %all-reduce.3.cloned.1.call-start = ((), (), s32[]{:S(2)}) async-start(), calls=%async_computation.8 | async-start | bytes 4194304 | tf_op jit(solution)/shard_map/psum | solution.py:123
  25.2 70.0 %copy-start.19 = (bf16[1280,128]{1,0:T(8,128)(2,1)S(1)}, bf16[1280,128]{1,0:T(8,128)(2,1)}, u32[]{:S(2)}) copy-start(bf16[1280,128]{1,0:T(8,128)(2,1)} %param.18) | copy-start | bytes 983044
  95.2 1.6 copy-start.20
  96.9 1.6 copy-start.10
  98.5 1.6 copy-start.9
  101.8 211.6 %reduce-scatter.2.cloned.1.call-start = ((), (), s32[]{:S(2)}) async-start(), calls=%async_computation.5 | async-start | bytes 13107200 | tf_op jit(solution)/shard_map/reduce_scatter | solution.py:142
  196.2 3.1 copy-start.6
  211.7 251.8 %all-gather.3.cloned.1.call-start = ((), (), s32[]{:S(2)}) async-start(), calls=%async_computation.6 | async-start | bytes 1392640 | tf_op jit(solution)/shard_map/all_gather | solution.py:41
  380.0 3.5 copy-start.18
  380.0 3.5 copy-start.22
  385.0 139.3 %all-gather.5.cloned.1.call-start = ((), (), s32[]{:S(2)}) async-start(), calls=%async_computation.7 | async-start | bytes 6553600 | tf_op jit(solution)/shard_map/all_gather | solution.py:41
  527.1 1.6 copy-start.4
  527.2 2.4 copy-start.2
  528.8 1.1 copy-start.7
  535.4 103.4 %all-to-all-start.3 = ((f32[4,1,262144]{2,1,0:T(1,128)}), f32[4,1,262144]{2,1,0:T(1,128)}, u32[]{:S(2)}, u32[]{:S(2)}) async-start(f32[4,1,262144]{2,1,0:T(1,128)} %broadcast_in_dim.45), calls=%async_computation.4 | async-start | bytes 8388608 | tf_op jit(solution)/shard_map/all_to_all | solution.py:17
  542.4 6.2 copy-start.8
  546.2 2.5 copy-start.5
  546.2 3.3 copy-start.13
  548.7 1.8 copy-start.3
  548.7 1.9 copy-start.12
  552.7 96.9 %copy-start.15 = (f32[1024,128]{1,0:T(8,128)S(1)}, f32[1024,128]{1,0:T(8,128)}, u32[]{:S(2)}) copy-start(f32[1024,128]{1,0:T(8,128)} %get-tuple-element.12) | copy-start | bytes 1572868
  649.6 2.5 copy-start.11
  649.6 2.5 copy-start.14
  649.6 2.5 copy-start.16
  649.6 2.5 copy-start.17
  649.6 2.5 copy-start.21
  652.1 1.1 copy-start.23
  652.1 1.3 copy-start.24
  653.4 2.4 copy-start.25
  653.4 2.4 copy-start.26
  655.7 2.4 copy-start.1
Sparse Core Ops, SparseCore 0:
  102.0 91.5 all-reduce.2
  211.8 101.5 reduce-scatter.1
  385.1 78.3 all-gather.2
  466.2 57.9 all-gather.4
